TPU v7x, 32 devices: a whole 2x2x4 slice. The times are simulated.
32 devices in a mesh: slab: 2 (over x), py: 4 (over y, core), px: 4 (over z).
Axes of the slice: x: 2, y: 2, z: 4, core: 2. Of those that a mesh axis runs over, the one named last changes fastest.
Arguments:
- state: bfloat16 [2, 3, 16, 1024, 1024], P(None, None, 'slab', ('py', 'px')), may hold values from -12 to 12
- shells: int32 [16, 1024, 1024], P('slab', ('py', 'px')), may hold values from 0 to 511
Outputs:
- restored: float32 [2, 3, 16, 1024, 1024], P(None, None, ('slab', 'py'), None, 'px')
- spectrum: float32 [512], replicated
All inputs are finite; a program needn't handle non-finite values.
Results may differ from a plain program's by a relative error of at most 0.0003.
Values may be sent and summed in bfloat16 or wider, within the bound.
A program may use at most 128 MiB of HBM per device.

v0:
```python
import math
import jax
import jax.numpy as jnp
from jax import lax
from jax.sharding import PartitionSpec as P

SHELLS = 512


def mode_energy(values):
    return 0.5 * jnp.sum(values * values, axis=(0, 1))


def bin_energy(energy, labels_in):
    flat_energy = energy.reshape(-1)
    flat_labels = labels_in.reshape(-1)
    mode_count = flat_energy.shape[0]
    block_len = math.gcd(mode_count, 16384)
    high_rows = SHELLS // 128
    energy_blocks = flat_energy.reshape(mode_count // block_len, block_len)
    label_blocks = flat_labels.reshape(mode_count // block_len, block_len)

    def add_block(running, pieces):
        values, labels = pieces
        upper = values.astype(jnp.bfloat16)
        remain = values - upper.astype(jnp.float32)
        middle = remain.astype(jnp.bfloat16)
        lower = (remain - middle.astype(jnp.float32)).astype(jnp.bfloat16)
        high_part = labels // 128
        low_part = labels % 128
        high_hot = (high_part[:, None] == jnp.arange(high_rows, dtype=jnp.int32)[None, :]).astype(
            jnp.bfloat16
        )
        weighted = jnp.concatenate(
            [high_hot * upper[:, None], high_hot * middle[:, None], high_hot * lower[:, None]],
            axis=1,
        )
        onehot = (low_part[:, None] == jnp.arange(128, dtype=jnp.int32)[None, :]).astype(
            jnp.bfloat16
        )
        partial_sum = lax.dot_general(
            weighted, onehot, (((0,), (0,)), ((), ())), preferred_element_type=jnp.float32
        )
        partial_sum = partial_sum.reshape(3, high_rows, 128)
        return (running + (partial_sum[0] + partial_sum[1] + partial_sum[2]), None)

    running, _ = lax.scan(
        add_block, jnp.zeros((high_rows, 128), jnp.float32), (energy_blocks, label_blocks)
    )
    return running.reshape(SHELLS)


def local(state, shells):
    py_count = lax.axis_size("py")
    px_count = lax.axis_size("px")
    planes = state.shape[2]
    rows_local = state.shape[3]
    columns = state.shape[4]
    planes_out = planes // py_count
    columns_out = columns // px_count
    sectioned = state.reshape(2, 3, planes, 1, 1, rows_local, columns)
    received = lax.all_to_all(
        lax.all_to_all(sectioned, "py", split_axis=2, concat_axis=3, tiled=True),
        "px",
        split_axis=6,
        concat_axis=4,
        tiled=True,
    )
    restored = received.reshape(
        2, 3, planes_out, rows_local * py_count * px_count, columns_out
    ).astype(jnp.float32)
    totals = bin_energy(mode_energy(state.astype(jnp.float32)), shells)
    modes_all = planes * rows_local * columns * lax.axis_size("slab") * py_count * px_count
    totals = lax.psum(totals, ("slab", "py", "px"))
    spectrum = totals * (SHELLS / modes_all)
    return (restored, spectrum)


def solution(mesh):
    return jax.shard_map(
        local,
        mesh=mesh,
        in_specs=(P(None, None, "slab", ("py", "px"), None), P("slab", ("py", "px"), None)),
        out_specs=(P(None, None, ("slab", "py"), None, "px"), P()),
        check_vma=False,
    )
```

profile of v0, /device:TPU:0, one launch (start us, length us, event | category | flops | bytes accessed | tf_op | source)
XLA Modules:
  0.0 352.4 jit_solution(16731340654529815363)
XLA Ops:
  0.6 6.7 %copy.16 = bf16[2,3,8,64,1024]{4,3,1,0,2:T(8,128)(2,1)} copy(bf16[2,3,8,64,1024]{4,3,2,1,0:T(8,128)(2,1)} %param.4) | data formatting | bytes 12582912 | tf_op args[0]
  7.4 5.3 %all-to-all-start = ((bf16[2,3,8,1,1,64,1024]{6,5,1,0,4,3,2:T(8,128)(2,1)}), bf16[2,3,8,1,1,64,1024]{6,5,1,0,4,3,2:T(8,128)(2,1)}, u32[]{:S(2)}, u32[]{:S(2)}) async-start(bf16[2,3,8,1,1,64,1024]{6,5,1,0,4,3,2:T(8,128)(2,1)} %bitcast.24), calls=%async_computation | async-start | bytes 12582912 | tf_op jit(solution)/shard_map/all_to_all | solution.py:63
  12.6 4.6 %multiply_reduce_fusion = f32[8,64,1024]{2,1,0:T(8,128)S(1)} fusion(bf16[2,3,8,64,1024]{4,3,2,1,0:T(8,128)(2,1)} %param.4), kind=kLoop, calls=%fused_computation.29 | loop fusion | flops 8912896 | bytes 8388608 | tf_op jit(solution)/shard_map/reduce_sum | solution.py:11
  17.4 1.5 mul.58
  19.0 1.7 reshape_reshape.4
  20.7 63.3 %all-to-all-done = bf16[2,3,8,1,1,64,1024]{6,5,1,0,4,3,2:T(8,128)(2,1)} async-done(((bf16[2,3,8,1,1,64,1024]{6,5,1,0,4,3,2:T(8,128)(2,1)}), bf16[2,3,8,1,1,64,1024]{6,5,1,0,4,3,2:T(8,128)(2,1)}, u32[]{:S(2)}, u32[]{:S(2)}) %all-to-all-start) | async-done | bytes 6291488 | tf_op jit(solution)/shard_map/all_to_all | solution.py:63
  84.0 20.1 %copy.12 = bf16[2,3,4,2,1,1,64,1024]{6,2,3,1,0,7,5,4:T(4,128)(2,1)} copy(bf16[2,3,4,2,1,1,64,1024]{7,6,1,0,3,2,5,4:T(8,128)(2,1)} %bitcast.1) | data formatting | bytes 12582912 | tf_op jit(solution)/shard_map/all_to_all | solution.py:63
  104.1 10.9 %bitcast_bitcast_fusion = bf16[1024,1,2,3,2,4,64]{6,5,4,3,2,1,0:T(4,128)(2,1)} fusion(bf16[2,3,4,2,1,1,64,1024]{6,2,3,1,0,7,5,4:T(4,128)(2,1)} %copy.12), kind=kLoop, calls=%fused_computation.33 | loop fusion | bytes 12582912
  115.0 12.8 %reshape.115 = bf16[4,2,393216]{2,1,0:T(2,128)(2,1)} reshape(bf16[1024,1,2,3,2,4,64]{6,5,4,3,2,1,0:T(4,128)(2,1)} %bitcast_bitcast_fusion) | data formatting | bytes 12582912
  127.8 5.7 %all-to-all-start.1 = ((bf16[4,2,393216]{2,1,0:T(2,128)(2,1)}), bf16[4,2,393216]{2,1,0:T(2,128)(2,1)}, u32[]{:S(2)}, u32[]{:S(2)}) async-start(bf16[4,2,393216]{2,1,0:T(2,128)(2,1)} %reshape.115), calls=%async_computation.1 | async-start | bytes 12582912 | tf_op jit(solution)/shard_map/all_to_all | solution.py:62
  133.5 122.2 %while.13 = (s32[]{:T(128)}, f32[4,128]{1,0:T(4,128)S(1)}, s32[32,16384]{1,0:T(8,128)S(1)}, f32[32,16384]{1,0:T(8,128)}, s32[]{:T(128)}, /*index=5*/s32[]{:T(128)}) while((s32[]{:T(128)}, f32[4,128]{1,0:T(4,128)S(1)}, s32[32,16384]{1,0:T(8,128)S(1)}, f32[32,16384]{1,0:T(8,128)}, s32[]{:T(128)}, /*index=5*/s32[]{:T(128)}) %tuple.44), condition=%wide.region_2.3_spmd.clone, body=%wide.region_1.2_spmd.clone.sunk | while | flops 54315008 | bytes 1720407 | solution.py:47
  134.9 2.3 fusion.23
  138.8 2.3 fusion.23
  142.6 2.3 fusion.23
  146.4 2.3 fusion.23
  150.2 2.3 fusion.23
  154.0 2.3 fusion.23
  157.9 2.3 fusion.23
  161.7 2.3 fusion.23
  165.5 2.3 fusion.23
  169.3 2.3 fusion.23
  173.1 2.3 fusion.23
  176.9 2.3 fusion.23
  180.8 2.3 fusion.23
  184.6 2.3 fusion.23
  188.4 2.3 fusion.23
  192.2 2.3 fusion.23
  196.0 2.3 fusion.23
  199.9 2.3 fusion.23
  203.7 2.3 fusion.23
  207.5 2.3 fusion.23
  211.3 2.3 fusion.23
  215.1 2.3 fusion.23
  219.0 2.3 fusion.23
  222.8 2.3 fusion.23
  226.6 2.3 fusion.23
  230.4 2.3 fusion.23
  234.2 2.3 fusion.23
  238.1 2.3 fusion.23
  241.9 2.3 fusion.23
  245.7 2.3 fusion.23
  249.5 2.3 fusion.23
  253.3 2.3 fusion.23
  255.7 40.2 %psum.7 = f32[512]{0:T(512)S(1)} all-reduce(f32[512]{0:T(512)S(1)} %bitcast.29), channel_id=1, replica_groups=mesh['slab'=2,'py'=4,'px'=4] {'slab','py','px'}, use_global_device_ids=true, to_apply=%region_3.4 | all-reduce | flops 512 | bytes 4096 | tf_op jit(solution)/shard_map/psum | solution.py:74
  296.5 12.7 %reshape.116 = bf16[1024,1,2,3,2,4,64]{6,5,4,3,2,1,0:T(4,128)(2,1)} reshape(bf16[4,2,393216]{2,1,0:T(2,128)(2,1)} %all-to-all-done.1) | data formatting | bytes 12582912
  309.2 18.5 %copy.13 = bf16[2,3,2,4,1,64,1024]{6,5,4,3,2,1,0:T(8,128)(2,1)} copy(bf16[2,3,2,4,1,64,1024]{5,3,2,1,0,4,6:T(4,128)(2,1)} %bitcast.22) | data formatting | bytes 12582912 | tf_op jit(solution)/shard_map/all_to_all | solution.py:62
  327.7 12.6 %reshape.114 = f32[2,3,2,4,1,64,4,256]{7,6,5,3,2,1,0,4:T(4,128)} reshape(bf16[2,3,2,4,1,64,1024]{6,5,4,3,2,1,0:T(8,128)(2,1)} %copy.13) | data formatting | bytes 18874368 | tf_op jit(solution)/shard_map/convert_element_type | solution.py:71
  340.3 12.0 %copy.14 = f32[2,3,2,4,4,1,64,256]{7,6,4,3,2,1,0,5:T(8,128)} copy(f32[2,3,2,4,4,1,64,256]{7,4,6,3,2,1,0,5:T(4,128)} %bitcast.23) | data formatting | bytes 25165824 | tf_op jit(solution)/shard_map/convert_element_type | solution.py:71
  (228 shorter events, 46.1 us)
Async XLA Ops:
  7.4 76.6 %all-to-all-start = ((bf16[2,3,8,1,1,64,1024]{6,5,1,0,4,3,2:T(8,128)(2,1)}), bf16[2,3,8,1,1,64,1024]{6,5,1,0,4,3,2:T(8,128)(2,1)}, u32[]{:S(2)}, u32[]{:S(2)}) async-start(bf16[2,3,8,1,1,64,1024]{6,5,1,0,4,3,2:T(8,128)(2,1)} %bitcast.24), calls=%async_computation | async-start | bytes 12582912 | tf_op jit(solution)/shard_map/all_to_all | solution.py:63
  127.8 168.7 %all-to-all-start.1 = ((bf16[4,2,393216]{2,1,0:T(2,128)(2,1)}), bf16[4,2,393216]{2,1,0:T(2,128)(2,1)}, u32[]{:S(2)}, u32[]{:S(2)}) async-start(bf16[4,2,393216]{2,1,0:T(2,128)(2,1)} %reshape.115), calls=%async_computation.1 | async-start | bytes 12582912 | tf_op jit(solution)/shard_map/all_to_all | solution.py:62
where the time goes:
time: 356 us; the launch traced here: 352 us
  local copies, waits for them, and re-layouts  146 us (41%)
  matrix products  74.9 us (21%)
  waiting for transfers between devices  63.3 us (18%)
  blocking collectives  40.2 us (11%)
  other arithmetic  14 us (4%)
  starting transfers between devices  10.9 us (3%)
    dot_general x32, matrix products, add_block(): lax.dot_general(weighted, onehot, (((0,), (0,)), ((), ())), preferred_ele...  74.9 us
    all_to_all x1, waiting for transfers between devices, local(): lax.all_to_all(sectioned, 'py', split_axis=2, concat_axis=3, tiled=True)  63.3 us
    unnamed x4, local copies, waits for them, and re-layouts  43.1 us
    psum x1, blocking collectives, local(): totals = lax.psum(totals, ('slab', 'py', 'px'))  40.2 us
    dynamic_slice x64, local copies, waits for them, and re-layouts, bin_energy(): lax.scan(add_block, jnp.zeros((high_rows, 128), jnp.float32), (energy_blo...  36.7 us
    convert_element_type x2, local copies, waits for them, and re-layouts, local(): restored = received.reshape(2, 3, planes_out, rows_local * py_count * px_...  24.7 us
    all_to_all x1, local copies, waits for them, and re-layouts, local(): lax.all_to_all(sectioned, 'py', split_axis=2, concat_axis=3, tiled=True)  20.1 us
    all_to_all x1, local copies, waits for them, and re-layouts, local(): lax.all_to_all(lax.all_to_all(sectioned, 'py', split_axis=2, concat_axis=...  18.5 us
  transfers between devices with their start and end apart: 2, of which 1 were waited for; matrix products, arithmetic and copies ran while one was open for 37% of the time, Pallas kernels for 0%

commit v1 on v0

--- a/solution.py
+++ b/solution.py
@@ -59,13 +59,10 @@
     planes_out = planes // py_count
     columns_out = columns // px_count
     sectioned = state.reshape(2, 3, planes, 1, 1, rows_local, columns)
-    received = lax.all_to_all(
-        lax.all_to_all(sectioned, "py", split_axis=2, concat_axis=3, tiled=True),
-        "px",
-        split_axis=6,
-        concat_axis=4,
-        tiled=True,
-    )
+    block = lax.all_to_all(sectioned, "py", split_axis=2, concat_axis=3, tiled=True)
+    shards = jnp.split(block, lax.axis_size("px"), axis=6)
+    got = lax.all_to_all(jnp.stack(shards), "px", 0, 0)
+    received = jnp.concatenate(got, axis=4)
     restored = received.reshape(
         2, 3, planes_out, rows_local * py_count * px_count, columns_out
     ).astype(jnp.float32)

time: 356 us -> 271 us (0.76)
  local copies, waits for them, and re-layouts: 146 us -> 51.2 us
  other arithmetic: 14 us -> 26.3 us
    unnamed x4 -> x1, local copies, waits for them, and re-layouts: 43.1 us -> 6.74 us
    convert_element_type x2 -> x0, local copies, waits for them, and re-layouts: 24.7 us -> none  [local(): restored = received.reshape(2, 3, planes_out, rows_local * py_count * px_...]
    all_to_all x1 -> x0, local copies, waits for them, and re-layouts: 18.5 us -> none  [local(): lax.all_to_all(lax.all_to_all(sectioned, 'py', split_axis=2, concat_axis=...]
    all_to_all x1, local copies, waits for them, and re-layouts: 20.1 us -> 3.49 us  [local(): lax.all_to_all(sectioned, 'py', split_axis=2, concat_axis=3, tiled=True)]
    convert_element_type x0 -> x1, other arithmetic: none -> 9.13 us  [local(): restored = received.reshape(2, 3, planes_out, rows_local * py_count * px_...]
  transfers between devices with their start and end apart: 2 -> 2, of which waited for: 1 -> 1; matrix products, arithmetic and copies ran while one was open for 37% -> 48% of each run, Pallas kernels for 0% -> 0%
where the time goes in v1:
time: 271 us; the launch traced here: 269 us
  matrix products  74.9 us (28%)
  waiting for transfers between devices  63.3 us (23%)
  local copies, waits for them, and re-layouts  51.2 us (19%)
  blocking collectives  40 us (15%)
  other arithmetic  26.3 us (10%)
  starting transfers between devices  10.9 us (4%)
    dot_general x32, matrix products, add_block(): lax.dot_general(weighted, onehot, (((0,), (0,)), ((), ())), preferred_ele...  74.9 us
    all_to_all x1, waiting for transfers between devices, local(): lax.all_to_all(sectioned, 'py', split_axis=2, concat_axis=3, tiled=True)  63.3 us
    psum x1, blocking collectives, local(): totals = lax.psum(totals, ('slab', 'py', 'px'))  40 us
    dynamic_slice x64, local copies, waits for them, and re-layouts, bin_energy(): lax.scan(add_block, jnp.zeros((high_rows, 128), jnp.float32), (energy_blo...  36.7 us
    convert_element_type x1, other arithmetic, local(): restored = received.reshape(2, 3, planes_out, rows_local * py_count * px_...  9.13 us
    unnamed x1, local copies, waits for them, and re-layouts  6.74 us
    all_to_all x1, starting transfers between devices, local(): got = lax.all_to_all(jnp.stack(shards), 'px', 0, 0)  5.67 us
    mul x32, other arithmetic, add_block(): high_hot * upper[:, None]  5.57 us
  transfers between devices with their start and end apart: 2, of which 1 were waited for; matrix products, arithmetic and copies ran while one was open for 48% of the time, Pallas kernels for 0%

profile of v1, /device:TPU:0, one launch (start us, length us, event | category | flops | bytes accessed | tf_op | source)
XLA Modules:
  0.0 269.2 jit_solution(14379471272853002307)
XLA Ops:
  0.6 6.7 %copy.17 = bf16[2,3,8,64,1024]{4,3,1,0,2:T(8,128)(2,1)} copy(bf16[2,3,8,64,1024]{4,3,2,1,0:T(8,128)(2,1)} %param.4) | data formatting | bytes 12582912 | tf_op args[0]
  7.4 5.3 %all-to-all-start = ((bf16[2,3,8,1,1,64,1024]{6,5,1,0,4,3,2:T(8,128)(2,1)}), bf16[2,3,8,1,1,64,1024]{6,5,1,0,4,3,2:T(8,128)(2,1)}, u32[]{:S(2)}, u32[]{:S(2)}) async-start(bf16[2,3,8,1,1,64,1024]{6,5,1,0,4,3,2:T(8,128)(2,1)} %bitcast.27), calls=%async_computation | async-start | bytes 12582912 | tf_op jit(solution)/shard_map/all_to_all | solution.py:62
  12.6 4.6 %multiply_reduce_fusion = f32[8,64,1024]{2,1,0:T(8,128)S(1)} fusion(bf16[2,3,8,64,1024]{4,3,2,1,0:T(8,128)(2,1)} %param.4), kind=kLoop, calls=%fused_computation.29 | loop fusion | flops 8912896 | bytes 8388608 | tf_op jit(solution)/shard_map/reduce_sum | solution.py:11
  17.4 1.6 mul.58
  19.0 1.7 reshape_reshape.2
  20.7 63.3 %all-to-all-done = bf16[2,3,8,1,1,64,1024]{6,5,1,0,4,3,2:T(8,128)(2,1)} async-done(((bf16[2,3,8,1,1,64,1024]{6,5,1,0,4,3,2:T(8,128)(2,1)}), bf16[2,3,8,1,1,64,1024]{6,5,1,0,4,3,2:T(8,128)(2,1)}, u32[]{:S(2)}, u32[]{:S(2)}) %all-to-all-start) | async-done | bytes 6291488 | tf_op jit(solution)/shard_map/all_to_all | solution.py:62
  84.0 3.5 %copy.16 = bf16[2,3,4,2,1,1,64,1024]{7,6,2,3,1,0,5,4:T(8,128)(2,1)S(1)} copy(bf16[2,3,4,2,1,1,64,1024]{7,6,1,0,3,2,5,4:T(8,128)(2,1)} %bitcast.1) | data formatting | bytes 12582912 | tf_op jit(solution)/shard_map/all_to_all | solution.py:62
  88.4 3.2 %pad_maximum_fusion = bf16[4,2,3,2,4,1,64,256]{7,6,4,3,2,1,5,0:T(8,128)(2,1)} fusion(bf16[1,2,3,2,4,1,64,256]{7,6,4,3,2,1,5,0:T(8,128)(2,1)S(1)} %get-tuple-element.90, bf16[1,2,3,2,4,1,64,256]{7,6,4,3,2,1,5,0:T(8,128)(2,1)S(1)} %get-tuple-element.91, bf16[1,2,3,2,4,1,64,256]{7,6,4,3,2,1,5,0:T(8,128)(2,1)S(1)} %get-tuple-element.92, ...), kind=kLoop, calls=%fused_computation.30 | loop fusion | flops 9437184 | bytes 12582912 | tf_op jit(solution)/shard_map/stack | solution.py:64
  91.5 5.7 %all-to-all-start.1 = ((bf16[4,2,3,2,4,1,64,256]{7,6,4,3,2,1,5,0:T(8,128)(2,1)}), bf16[4,2,3,2,4,1,64,256]{7,6,4,3,2,1,5,0:T(8,128)(2,1)}, u32[]{:S(2)}, u32[]{:S(2)}) async-start(bf16[4,2,3,2,4,1,64,256]{7,6,4,3,2,1,5,0:T(8,128)(2,1)} %pad_maximum_fusion), calls=%async_computation.1 | async-start | bytes 12582912 | tf_op jit(solution)/shard_map/all_to_all | solution.py:64
  97.2 122.2 %while.13 = (s32[]{:T(128)}, f32[4,128]{1,0:T(4,128)S(1)}, s32[32,16384]{1,0:T(8,128)S(1)}, f32[32,16384]{1,0:T(8,128)}, s32[]{:T(128)}, /*index=5*/s32[]{:T(128)}) while((s32[]{:T(128)}, f32[4,128]{1,0:T(4,128)S(1)}, s32[32,16384]{1,0:T(8,128)S(1)}, f32[32,16384]{1,0:T(8,128)}, s32[]{:T(128)}, /*index=5*/s32[]{:T(128)}) %tuple.47), condition=%wide.region_2.3_spmd.clone, body=%wide.region_1.2_spmd.clone.sunk | while | flops 54315008 | bytes 1720407 | solution.py:47
  98.7 2.3 fusion.23
  101.0 1.1 constant_dynamic-slice_fusion.5
  102.5 2.3 fusion.23
  104.9 1.1 constant_dynamic-slice_fusion.5
  106.3 2.3 fusion.23
  108.7 1.1 constant_dynamic-slice_fusion.5
  110.1 2.3 fusion.23
  112.5 1.1 constant_dynamic-slice_fusion.5
  113.9 2.3 fusion.23
  117.8 2.3 fusion.23
  121.6 2.3 fusion.23
  125.4 2.3 fusion.23
  129.2 2.3 fusion.23
  133.0 2.3 fusion.23
  136.8 2.3 fusion.23
  140.7 2.3 fusion.23
  144.5 2.3 fusion.23
  148.3 2.3 fusion.23
  152.1 2.3 fusion.23
  155.9 2.3 fusion.23
  159.8 2.3 fusion.23
  163.6 2.3 fusion.23
  167.4 2.3 fusion.23
  171.2 2.3 fusion.23
  175.0 2.3 fusion.23
  178.9 2.3 fusion.23
  182.7 2.3 fusion.23
  186.5 2.3 fusion.23
  190.3 2.3 fusion.23
  194.1 2.3 fusion.23
  198.0 2.3 fusion.23
  201.8 2.3 fusion.23
  205.6 2.3 fusion.23
  209.4 2.3 fusion.23
  213.2 2.3 fusion.23
  217.1 2.3 fusion.23
  219.4 40.0 %psum.7 = f32[512]{0:T(512)S(1)} all-reduce(f32[512]{0:T(512)S(1)} %bitcast.33), channel_id=1, replica_groups=mesh['slab'=2,'py'=4,'px'=4] {'slab','py','px'}, use_global_device_ids=true, to_apply=%region_3.4 | all-reduce | flops 512 | bytes 4096 | tf_op jit(solution)/shard_map/psum | solution.py:71
  260.1 9.1 %copy_convert_fusion = f32[4,2,3,2,4,1,64,256]{7,6,0,4,3,2,1,5:T(8,128)} fusion(bf16[4,2,3,2,4,1,64,256]{7,6,4,3,2,1,5,0:T(8,128)(2,1)} %all-to-all-done.1), kind=kLoop, calls=%fused_computation.31 | loop fusion | flops 3145728 | bytes 18874368 | tf_op jit(solution)/shard_map/convert_element_type | solution.py:68
  (225 shorter events, 42.6 us)
Async XLA Ops:
  7.4 76.6 %all-to-all-start = ((bf16[2,3,8,1,1,64,1024]{6,5,1,0,4,3,2:T(8,128)(2,1)}), bf16[2,3,8,1,1,64,1024]{6,5,1,0,4,3,2:T(8,128)(2,1)}, u32[]{:S(2)}, u32[]{:S(2)}) async-start(bf16[2,3,8,1,1,64,1024]{6,5,1,0,4,3,2:T(8,128)(2,1)} %bitcast.27), calls=%async_computation | async-start | bytes 12582912 | tf_op jit(solution)/shard_map/all_to_all | solution.py:62
  91.5 168.5 %all-to-all-start.1 = ((bf16[4,2,3,2,4,1,64,256]{7,6,4,3,2,1,5,0:T(8,128)(2,1)}), bf16[4,2,3,2,4,1,64,256]{7,6,4,3,2,1,5,0:T(8,128)(2,1)}, u32[]{:S(2)}, u32[]{:S(2)}) async-start(bf16[4,2,3,2,4,1,64,256]{7,6,4,3,2,1,5,0:T(8,128)(2,1)} %pad_maximum_fusion), calls=%async_computation.1 | async-start | bytes 12582912 | tf_op jit(solution)/shard_map/all_to_all | solution.py:64
